TPU v7x, 32 devices: a whole 2x2x4 slice. The times are simulated.
32 devices in a mesh: dp: 8 (over z, y), section: 4 (over x, core).
Axes of the slice: x: 2, y: 2, z: 4, core: 2. Of those that a mesh axis runs over, the one named last changes fastest.
Arguments:
- slot_of_token: int32 [2, 1, 1024], P(None, None, 'dp'), may hold values from -1 to 127, as said below
- gate_prob: float32 [2, 1, 1024], P(None, None, 'dp'), may hold values from 0.2 to 1
- layer_input: bfloat16 [1, 1024, 7168], P(None, 'dp', 'section'), may hold values from -6 to 6
- preact: bfloat16 [1, 1024, 2048], P(None, 'dp', 'section'), may hold values from -6 to 6
- top_grad: bfloat16 [1, 1024, 3584], P(None, 'dp'), may hold values from -6 to 6
- w_up: bfloat16 [1024, 7168], P('dp', 'section'), may hold values from -0.09375 to 0.09375
- w_down: bfloat16 [1024, 7168], P('dp', 'section'), may hold values from -0.1875 to 0.1875
Outputs:
- grad_inputs: bfloat16 [1, 1024, 7168], P(None, 'dp', 'section')
- grad_up: float32 [1024, 7168], P('dp', 'section')
- grad_down: float32 [1024, 7168], P('dp', 'section')
Inputs may be any that keep to these rules, and one draw needn't show every extreme that they name: `slot_of_token`: within one layer, one micro-batch and the 128 tokens of one data replica, the values other than -1 are distinct; -1 marks a token that is not routed to the expert or dropped.
All inputs are finite; a program needn't handle non-finite values.
Results may differ from a plain program's by a relative error of at most 0.0098.
Values may be sent and summed in bfloat16 or wider, within the bound.
No kernel may reach another device: no remote copies, remote signals or barrier semaphores. Data moves between devices by JAX's collectives and lax.ppermute only.
A program may use at most 128 MiB of HBM per device.

v0:
```python
import jax
import jax.numpy as jnp
from jax import lax
from jax.sharding import PartitionSpec as P


def swapped(block, axis, apart):
    count = lax.axis_size(axis)
    route = []
    for low in range(count):
        high = low | 1 << apart
        if high != low and high < count:
            route += [(low, high), (high, low)]
    return lax.ppermute(block, axis, route)


def passed_along(shard, axis, by):
    count = lax.axis_size(axis)
    pairs = [(i, i + by) for i in range(count) if 0 <= i + by < count]
    return lax.ppermute(shard, axis, pairs)


def silu_slope(pre):
    sigmoid_val = jax.nn.sigmoid(pre)
    return sigmoid_val * (1.0 + pre * (1.0 - sigmoid_val))


def pick(stack, index):
    return lax.dynamic_index_in_dim(stack, index, 0, keepdims=False)


def local(slot_of_token, gate_prob, layer_input, preact, top_grad, w_up, w_down):
    micro_count = layer_input.shape[0]
    token_rows = layer_input.shape[1]
    half_width = layer_input.shape[2]
    slot_count = preact.shape[1]
    section_index = lax.axis_index("section")
    pair_index = section_index // 2
    core_index = section_index % 2
    layer_count = lax.axis_size("section") // 2
    up_half, down_half = (
        lax.all_gather(w_up, "dp", axis=0, tiled=True),
        lax.all_gather(w_down, "dp", axis=0, tiled=True),
    )
    hidden_units = up_half.shape[0]
    other_pre = swapped(preact, "section", 0)
    pre_full = jnp.where(
        core_index == 0,
        jnp.concatenate([preact, other_pre], 2),
        jnp.concatenate([other_pre, preact], 2),
    ).astype(jnp.float32)
    slope_all = silu_slope(pre_full)
    hidden_all = jax.nn.silu(pre_full).astype(jnp.bfloat16)
    slots_here = pick(slot_of_token, pair_index)
    gates_here = pick(gate_prob, pair_index)
    slot_ids = jnp.arange(slot_count, dtype=jnp.int32)
    onehot_all = (slots_here[:, None, :] == slot_ids[None, :, None]).astype(jnp.bfloat16)
    slot_inputs = jnp.einsum(
        "mst,mtd->msd", onehot_all, layer_input, preferred_element_type=jnp.float32
    ).astype(jnp.bfloat16)
    top_half = lax.dynamic_slice_in_dim(top_grad, core_index * half_width, half_width, 2)
    tick_count = micro_count + layer_count - 1
    received = jnp.zeros((token_rows, half_width), jnp.bfloat16)
    grad_inputs = jnp.zeros_like(layer_input)
    pre_grads = jnp.zeros((micro_count, slot_count, hidden_units), jnp.bfloat16)
    slot_grads = jnp.zeros((micro_count, slot_count, half_width), jnp.bfloat16)
    for step_index in range(tick_count):
        micro_raw = step_index - (layer_count - 1 - pair_index)
        active = (micro_raw >= 0) & (micro_raw < micro_count)
        micro_now = jnp.clip(micro_raw, 0, micro_count - 1)
        incoming = jnp.where(pair_index == layer_count - 1, pick(top_half, micro_now), received)
        onehot = pick(onehot_all, micro_now)
        scaled = (pick(gates_here, micro_now)[:, None] * incoming.astype(jnp.float32)).astype(
            jnp.bfloat16
        )
        slot_grad = jnp.dot(onehot, scaled, preferred_element_type=jnp.float32).astype(jnp.bfloat16)
        partial_grad = lax.dot_general(
            slot_grad, down_half, (((1,), (1,)), ((), ())), preferred_element_type=jnp.float32
        )
        other_grad = swapped(partial_grad, "section", 0)
        hidden_grad = partial_grad + other_grad
        pre_grad = (hidden_grad * pick(slope_all, micro_now)).astype(jnp.bfloat16)
        slot_input_grad = jnp.dot(pre_grad, up_half, preferred_element_type=jnp.float32).astype(
            jnp.bfloat16
        )
        delta = lax.dot_general(
            onehot, slot_input_grad, (((0,), (0,)), ((), ())), preferred_element_type=jnp.float32
        )
        grad_new = (incoming.astype(jnp.float32) + delta).astype(jnp.bfloat16)
        grad_inputs = lax.dynamic_update_index_in_dim(
            grad_inputs, jnp.where(active, grad_new, pick(grad_inputs, micro_now)), micro_now, 0
        )
        pre_grads = lax.dynamic_update_index_in_dim(
            pre_grads, jnp.where(active, pre_grad, pick(pre_grads, micro_now)), micro_now, 0
        )
        slot_grads = lax.dynamic_update_index_in_dim(
            slot_grads, jnp.where(active, slot_grad, pick(slot_grads, micro_now)), micro_now, 0
        )
        received = passed_along(grad_new, "section", -2)
    up_rows = jnp.einsum("msf,msd->fd", pre_grads, slot_inputs, preferred_element_type=jnp.float32)
    down_rows = jnp.einsum(
        "msf,msd->fd", hidden_all, slot_grads, preferred_element_type=jnp.float32
    )
    summed = lax.psum_scatter(
        jnp.concatenate([up_rows, down_rows], 1), "dp", scatter_dimension=0, tiled=True
    )
    grad_up = summed[:, :half_width]
    grad_down = summed[:, half_width:]
    return (grad_inputs, grad_up, grad_down)


def solution(mesh):
    in_specs = (
        P(None, None, "dp"),
        P(None, None, "dp"),
        P(None, "dp", "section"),
        P(None, "dp", "section"),
        P(None, "dp", None),
        P("dp", "section"),
        P("dp", "section"),
    )
    out_specs = (P(None, "dp", "section"), P("dp", "section"), P("dp", "section"))
    return jax.shard_map(local, mesh=mesh, in_specs=in_specs, out_specs=out_specs, check_vma=False)
```

profile of v0, /device:TPU:0, one launch (start us, length us, event | category | flops | bytes accessed | tf_op | source)
XLA Modules:
  0.0 433.4 jit_solution(3888123693103680271)
XLA Ops:
  7.2 0.0 copy-start
  7.2 0.0 all-gather.3.cloned.1.call-start
  7.2 0.7 all-gather.3.cloned.1.call-update
  7.9 0.0 all-gather.5.cloned.1.call-start
  8.0 0.7 all-gather.5.cloned.1.call-update
  8.7 0.0 reduce-scatter.2.cloned.1.call-start
  8.8 0.7 fusion.44
  9.5 0.7 fusion.45
  10.1 1.4 convolution_convert_fusion.4
  11.5 67.6 %all-gather.3.cloned.1.call-done = bf16[1024,1792]{1,0:T(8,128)(2,1)} async-done(((bf16[128,1792]{1,0:T(8,128)(2,1)}), bf16[1024,1792]{1,0:T(8,128)(2,1)}) %all-gather.3.cloned.1.call-update) | async-done | bytes 3670032 | tf_op jit(solution)/shard_map/all_gather | solution.py:43
  79.2 3.3 fusion.51
  82.5 0.1 collective-permute-start
  82.6 0.5 collective-permute-start.1
  83.1 1.6 collective-permute-done.1
  84.7 1.3 multiply_convert_fusion.2
  86.0 60.3 %all-gather.5.cloned.1.call-done = bf16[1024,1792]{1,0:T(8,128)(2,1)} async-done(((bf16[128,1792]{1,0:T(8,128)(2,1)}), bf16[1024,1792]{1,0:T(8,128)(2,1)}) %all-gather.5.cloned.1.call-update) | async-done | bytes 3670032 | tf_op jit(solution)/shard_map/all_gather | solution.py:42
  146.3 2.9 fusion
  149.2 1.3 collective-permute-start.2
  150.5 11.2 %collective-permute-done.2 = bf16[128,1792]{1,0:T(8,128)(2,1)S(1)} collective-permute-done((bf16[128,1792]{1,0:T(8,128)(2,1)S(1)}, bf16[128,1792]{1,0:T(8,128)(2,1)S(1)}, u32[]{:S(2)}, u32[]{:S(2)}) %collective-permute-start.2) | collective-permute-done | bytes 458784 | tf_op jit(solution)/shard_map/ppermute | solution.py:20
  161.7 0.8 copy-done.2
  162.5 0.3 convolution_convert_fusion.3
  162.8 3.3 fusion.52
  166.2 0.1 collective-permute-start.3
  166.3 5.3 %fusion.17 = f32[1024,1792]{1,0:T(8,128)} fusion(bf16[128,1792]{1,0:T(8,128)(2,1)S(1)} %convolution_convert_fusion.3, bf16[128,1792]{1,0:T(8,128)(2,1)S(1)} %convolution_convert_fusion.4, pred[]{:T(512)S(6)} %and.20, pred[]{:T(512)S(6)} %and.18, bf16[128,512]{1,0:T(8,128)(2,1)} %bitcast.37, bf16[128,512]{1,0:T(8,128)(2,1)} %bitcast.33, pred[]{:T(512)S(6)} %eq.36), kind=kOutput, calls=%fused_computation.31 | convolution fusion | flops 472186880 | bytes 8519683 | tf_op jit(solution)/shard_map/msf,msd->fd/dot_general | solution.py:101
  171.6 1.3 multiply_convert_fusion.1
  172.9 4.2 fusion.4
  177.1 10.7 %pad_maximum_fusion = f32[1024,3584]{1,0:T(8,128)} fusion(f32[1024,1792]{1,0:T(8,128)} %fusion.17, f32[1024,1792]{1,0:T(8,128)} %fusion.4), kind=kLoop, calls=%fused_computation | loop fusion | flops 3670016 | bytes 29360128 | tf_op jit(solution)/shard_map/concatenate | solution.py:105
  187.8 0.0 reduce-scatter.2.cloned.1.call-update
  187.8 1.0 copy-done.3
  188.8 3.7 fusion.3
  192.5 231.6 %reduce-scatter.2.cloned.1.call-done = f32[128,3584]{1,0:T(8,128)} async-done(((f32[1024,3584]{1,0:T(8,128)}), f32[128,3584]{1,0:T(8,128)}) %reduce-scatter.2.cloned.1.call-update) | async-done | bytes 1835024 | tf_op jit(solution)/shard_map/reduce_scatter | solution.py:104
  424.1 2.8 fusion.50
  (15 shorter events, 0.0 us)
Async XLA Ops:
  7.2 165.7 %copy-start = (bf16[1,128,1792]{2,1,0:T(8,128)(2,1)S(1)}, bf16[1,128,1792]{2,1,0:T(8,128)(2,1)}, u32[]{:S(2)}) copy-start(bf16[1,128,1792]{2,1,0:T(8,128)(2,1)} %param.9) | copy-start | bytes 1376260
  7.2 75.4 %copy-start.4 = (bf16[1,128,512]{2,1,0:T(8,128)(2,1)S(1)}, bf16[1,128,512]{2,1,0:T(8,128)(2,1)}, u32[]{:S(2)}) copy-start(bf16[1,128,512]{2,1,0:T(8,128)(2,1)} %param.10) | copy-start | bytes 393220
  7.2 72.0 %all-gather.3.cloned.1.call-start = ((), (), s32[]{:S(2)}) async-start(), calls=%async_computation.1 | async-start | bytes 4128768 | tf_op jit(solution)/shard_map/all_gather | solution.py:43
  7.9 138.4 %all-gather.5.cloned.1.call-start = ((), (), s32[]{:S(2)}) async-start(), calls=%async_computation.2 | async-start | bytes 4128768 | tf_op jit(solution)/shard_map/all_gather | solution.py:42
  8.7 137.6 %copy-start.1 = (bf16[1,128,3584]{2,1,0:T(8,128)(2,1)S(1)}, bf16[1,128,3584]{2,1,0:T(8,128)(2,1)}, u32[]{:S(2)}) copy-start(bf16[1,128,3584]{2,1,0:T(8,128)(2,1)} %param.11) | copy-start | bytes 2752516
  8.7 415.4 %reduce-scatter.2.cloned.1.call-start = ((), (), s32[]{:S(2)}) async-start(), calls=%async_computation.3 | async-start | bytes 16515072 | tf_op jit(solution)/shard_map/reduce_scatter | solution.py:104
  82.5 2.2 collective-permute-start
  82.6 2.1 collective-permute-start.1
  84.7 65.8 %copy-start.6 = (bf16[1,128,512]{2,1,0:T(8,128)(2,1)}, bf16[1,128,512]{2,1,0:T(8,128)(2,1)S(1)}, u32[]{:S(2)}) copy-start(bf16[1,128,512]{2,1,0:T(8,128)(2,1)S(1)} %collective-permute-done.1) | copy-start | bytes 393220
  149.2 12.5 %collective-permute-start.2 = (bf16[128,1792]{1,0:T(8,128)(2,1)S(1)}, bf16[128,1792]{1,0:T(8,128)(2,1)S(1)}, u32[]{:S(2)}, u32[]{:S(2)}) collective-permute-start(bf16[128,1792]{1,0:T(8,128)(2,1)S(1)} %fusion), channel_id=1, source_target_pairs={{2,0},{3,1},{6,4},{7,5},{10,8},{11,9},{14,12},{15,13},{18,16},{19,... | collective-permute-start | bytes 1376264 | tf_op jit(solution)/shard_map/ppermute | solution.py:20
  161.7 0.8 copy-start.2
  166.2 5.4 %collective-permute-start.3 = (f32[128,1024]{1,0:T(8,128)S(1)}, f32[128,1024]{1,0:T(8,128)}, u32[]{:S(2)}, u32[]{:S(2)}) collective-permute-start(f32[128,1024]{1,0:T(8,128)S(1)} %fusion.52), channel_id=1, source_target_pairs={{0,1},{1,0},{2,3},{3,2},{4,5},{5,4},{6,7},{7,6},{8,9},{9,8},{10,11... | collective-permute-start | bytes 1572872 | tf_op jit(solution)/shard_map/ppermute | solution.py:14
  166.3 5.3 %copy-start.5 = (bf16[1,128,512]{2,1,0:T(8,128)(2,1)S(1)}, bf16[1,128,512]{2,1,0:T(8,128)(2,1)}, u32[]{:S(2)}) copy-start(bf16[1,128,512]{2,1,0:T(8,128)(2,1)} %param.10) | copy-start | bytes 393220
  166.3 5.3 %copy-start.7 = (bf16[1,128,512]{2,1,0:T(8,128)(2,1)S(1)}, bf16[1,128,512]{2,1,0:T(8,128)(2,1)}, u32[]{:S(2)}) copy-start(bf16[1,128,512]{2,1,0:T(8,128)(2,1)} %copy-done.6) | copy-start | bytes 393220
  187.8 1.0 copy-start.3
Sparse Core Ops, SparseCore 0:
  10.2 68.9 all-gather.2
  81.3 64.9 all-gather.4
  187.9 236.0 reduce-scatter.1
where the time goes:
time: 434 us; the launch traced here: 433 us
  waiting for transfers between devices  374 us (86%)
  matrix products  24.5 us (6%)
  between operations  13.9 us (3%)
  other arithmetic  13.3 us (3%)
  local copies, waits for them, and re-layouts  5.98 us (1%)
    reduce_scatter x1, waiting for transfers between devices, local(): lax.psum_scatter(jnp.concatenate([up_rows, down_rows], 1), 'dp', scatter_...  232 us
    all_gather x1, waiting for transfers between devices, local(): lax.all_gather(w_down, 'dp', axis=0, tiled=True)  67.6 us
    all_gather x1, waiting for transfers between devices, local(): lax.all_gather(w_up, 'dp', axis=0, tiled=True)  60.3 us
    ppermute x1, waiting for transfers between devices, passed_along(): return lax.ppermute(shard, axis, pairs)  11.2 us
    concatenate x1, other arithmetic, local(): jnp.concatenate([up_rows, down_rows], 1)  10.7 us
  transfers between devices with their start and end apart: 7, of which 5 were waited for; matrix products, arithmetic and copies ran while one was open for 4% of the time, Pallas kernels for 0%

commit v1 on v0

--- a/solution.py
+++ b/solution.py
@@ -29,6 +29,66 @@
     return lax.dynamic_index_in_dim(stack, index, 0, keepdims=False)
 
 
+def blocks_to_owners(blocks):
+    return lax.all_to_all(blocks, "dp", 0, 0, tiled=True)
+
+
+def column_blocks(x):
+    count = lax.axis_size("dp")
+    split = x.reshape(x.shape[:-1] + (count, x.shape[-1] // count))
+    return jnp.moveaxis(split, -2, 0)
+
+
+def to_every(x):
+    return jnp.broadcast_to(x[None], (lax.axis_size("dp"),) + x.shape)
+
+
+def both_halves(mine, core_index):
+    other = swapped(mine, "section", 0)
+    return jnp.where(
+        core_index == 0,
+        jnp.concatenate([mine, other], -1),
+        jnp.concatenate([other, mine], -1),
+    )
+
+
+def ring_order(count):
+    width = 1 << ((count.bit_length() - 1) // 2)
+    depth = count // width
+    order = [z * width for z in range(depth)]
+    for z in reversed(range(depth)):
+        steps = list(range(1, width))
+        order += [z * width + y for y in (steps if (depth - z) % 2 else steps[::-1])]
+    return order
+
+
+def ring_gather(shard):
+    count = lax.axis_size("dp")
+    order = ring_order(count)
+    place = [0] * count
+    for position, index in enumerate(order):
+        place[index] = position
+    here = jnp.asarray(place)[lax.axis_index("dp")]
+    order_table = jnp.asarray(order)
+    rows = shard.shape[0]
+    half = rows // 2
+    out = jnp.zeros((count, rows) + shard.shape[1:], shard.dtype)
+    out = lax.dynamic_update_slice(out, shard[None], (lax.axis_index("dp"), 0, 0))
+    ahead, behind = shard[:half], shard[half:]
+    forth = [(order[k], order[(k + 1) % count]) for k in range(count)]
+    back = [(high, low) for low, high in forth]
+    for step in range(1, count):
+        ahead = lax.ppermute(ahead, "dp", forth)
+        behind = lax.ppermute(behind, "dp", back)
+        out = lax.dynamic_update_slice(
+            out, ahead[None], (order_table[(here - step) % count], 0, 0)
+        )
+        out = lax.dynamic_update_slice(
+            out, behind[None], (order_table[(here + step) % count], half, 0)
+        )
+    return out.reshape((count * rows,) + shard.shape[1:])
+
+
 def local(slot_of_token, gate_prob, layer_input, preact, top_grad, w_up, w_down):
     micro_count = layer_input.shape[0]
     token_rows = layer_input.shape[1]
@@ -39,18 +99,13 @@
     core_index = section_index % 2
     layer_count = lax.axis_size("section") // 2
     up_half, down_half = (
-        lax.all_gather(w_up, "dp", axis=0, tiled=True),
-        lax.all_gather(w_down, "dp", axis=0, tiled=True),
+        ring_gather(w_up),
+        ring_gather(w_down),
     )
     hidden_units = up_half.shape[0]
-    other_pre = swapped(preact, "section", 0)
-    pre_full = jnp.where(
-        core_index == 0,
-        jnp.concatenate([preact, other_pre], 2),
-        jnp.concatenate([other_pre, preact], 2),
-    ).astype(jnp.float32)
-    slope_all = silu_slope(pre_full)
-    hidden_all = jax.nn.silu(pre_full).astype(jnp.bfloat16)
+    pre_width = preact.shape[2]
+    slope_all = silu_slope(both_halves(preact, core_index).astype(jnp.float32))
+    hidden_here = jax.nn.silu(preact.astype(jnp.float32)).astype(jnp.bfloat16)
     slots_here = pick(slot_of_token, pair_index)
     gates_here = pick(gate_prob, pair_index)
     slot_ids = jnp.arange(slot_count, dtype=jnp.int32)
@@ -58,6 +113,10 @@
     slot_inputs = jnp.einsum(
         "mst,mtd->msd", onehot_all, layer_input, preferred_element_type=jnp.float32
     ).astype(jnp.bfloat16)
+    early = blocks_to_owners(
+        jnp.concatenate([to_every(hidden_here), column_blocks(slot_inputs)], -1)
+    )
+    hidden_every = both_halves(early[..., :pre_width], core_index)
     top_half = lax.dynamic_slice_in_dim(top_grad, core_index * half_width, half_width, 2)
     tick_count = micro_count + layer_count - 1
     received = jnp.zeros((token_rows, half_width), jnp.bfloat16)
@@ -97,15 +156,24 @@
             slot_grads, jnp.where(active, slot_grad, pick(slot_grads, micro_now)), micro_now, 0
         )
         received = passed_along(grad_new, "section", -2)
-    up_rows = jnp.einsum("msf,msd->fd", pre_grads, slot_inputs, preferred_element_type=jnp.float32)
-    down_rows = jnp.einsum(
-        "msf,msd->fd", hidden_all, slot_grads, preferred_element_type=jnp.float32
+    pre_here = lax.dynamic_slice_in_dim(pre_grads, core_index * pre_width, pre_width, 2)
+    late = blocks_to_owners(
+        jnp.concatenate([to_every(pre_here), column_blocks(slot_grads)], -1)
     )
-    summed = lax.psum_scatter(
-        jnp.concatenate([up_rows, down_rows], 1), "dp", scatter_dimension=0, tiled=True
+    pre_every = both_halves(late[..., :pre_width], core_index)
+    up_columns = jnp.einsum(
+        "nmsf,nmsd->fd", pre_every, early[..., pre_width:], preferred_element_type=jnp.float32
     )
-    grad_up = summed[:, :half_width]
-    grad_down = summed[:, half_width:]
+    down_columns = jnp.einsum(
+        "nmsf,nmsd->fd", hidden_every, late[..., pre_width:], preferred_element_type=jnp.float32
+    )
+    columns = jnp.concatenate([up_columns, down_columns], 1).astype(jnp.bfloat16)
+    replicas = lax.axis_size("dp")
+    owned = blocks_to_owners(columns.reshape(replicas, hidden_units // replicas, -1))
+    owned = jnp.moveaxis(owned, 0, 1).astype(jnp.float32)
+    block_width = half_width // replicas
+    grad_up = owned[..., :block_width].reshape(-1, half_width)
+    grad_down = owned[..., block_width:].reshape(-1, half_width)
     return (grad_inputs, grad_up, grad_down)
 
 

time: 434 us -> 241 us (0.56)
  waiting for transfers between devices: 374 us -> 85.6 us
  starting transfers between devices: 2.04 us -> 46 us
  local copies, waits for them, and re-layouts: 5.98 us -> 43.1 us
  between operations: 13.9 us -> 37.4 us
  matrix products: 24.5 us -> 18 us
    reduce_scatter x1 -> x0, waiting for transfers between devices: 232 us -> none  [local(): lax.psum_scatter(jnp.concatenate([up_rows, down_rows], 1), 'dp', scatter_...]
    all_gather x2 -> x0, waiting for transfers between devices: 128 us -> none  [the longest x1 67.6 us: local(): lax.all_gather(w_down, 'dp', axis=0, tiled=True)]
    all_to_all x0 -> x3, waiting for transfers between devices: none -> 53.4 us  [blocks_to_owners(): return lax.all_to_all(blocks, 'dp', 0, 0, tiled=True)]
    ppermute x0 -> x28, starting transfers between devices: none -> 29.5 us  [the longest x14 28.5 us: ring_gather(): ahead = lax.ppermute(ahead, 'dp', forth)]
    dynamic_update_slice x0 -> x30, local copies, waits for them, and re-layouts: none -> 25.1 us  [the longest x14 11.7 us: ring_gather(): lax.dynamic_update_slice(out, behind[None], (order_table[(here + step) %...]
    ppermute x0 -> x28, waiting for transfers between devices: none -> 17.7 us  [the longest x14 16.8 us: ring_gather(): ahead = lax.ppermute(ahead, 'dp', forth)]
    all_to_all x0 -> x3, starting transfers between devices: none -> 15 us  [blocks_to_owners(): return lax.all_to_all(blocks, 'dp', 0, 0, tiled=True)]
    dot_general x2 -> x3, matrix products: 9.54 us -> 1.85 us  [the longest x1 0.79 us: local(): jnp.einsum('nmsf,nmsd->fd', pre_every, early[..., pre_width:], preferred_...]
  transfers between devices with their start and end apart: 7 -> 37, of which waited for: 5 -> 18; matrix products, arithmetic and copies ran while one was open for 4% -> 26% of each run, Pallas kernels for 0% -> 0%
where the time goes in v1:
time: 241 us; the launch traced here: 239 us
  waiting for transfers between devices  85.6 us (36%)
  starting transfers between devices  46 us (19%)
  local copies, waits for them, and re-layouts  43.1 us (18%)
  between operations  37.4 us (16%)
  matrix products  18 us (7%)
  other arithmetic  9.11 us (4%)
    all_to_all x3, waiting for transfers between devices, blocks_to_owners(): return lax.all_to_all(blocks, 'dp', 0, 0, tiled=True)  53.4 us
    ppermute x14, starting transfers between devices, ring_gather(): ahead = lax.ppermute(ahead, 'dp', forth)  28.5 us
    ppermute x14, waiting for transfers between devices, ring_gather(): ahead = lax.ppermute(ahead, 'dp', forth)  16.8 us
    all_to_all x3, starting transfers between devices, blocks_to_owners(): return lax.all_to_all(blocks, 'dp', 0, 0, tiled=True)  15 us
    ppermute x1, waiting for transfers between devices, passed_along(): return lax.ppermute(shard, axis, pairs)  13.2 us
    dynamic_update_slice x14, local copies, waits for them, and re-layouts, ring_gather(): lax.dynamic_update_slice(out, behind[None], (order_table[(here + step) %...  11.7 us
    dynamic_update_slice x14, local copies, waits for them, and re-layouts, ring_gather(): lax.dynamic_update_slice(out, ahead[None], (order_table[(here - step) % c...  11.7 us
    dot_general x2, matrix products, local(): lax.dot_general(onehot, slot_input_grad, (((0,), (0,)), ((), ())), prefer...  6.89 us
  transfers between devices with their start and end apart: 37, of which 18 were waited for; matrix products, arithmetic and copies ran while one was open for 26% of the time, Pallas kernels for 0%

profile of v1, /device:TPU:0, one launch (start us, length us, event | category | flops | bytes accessed | tf_op | source)
XLA Modules:
  0.0 239.3 jit_solution(10144162119306618826)
XLA Ops:
  2.5 3.1 %collective-permute-start.16 = (bf16[64,1792]{1,0:T(8,128)(2,1)}, bf16[64,1792]{1,0:T(8,128)(2,1)}, u32[]{:S(2)}, u32[]{:S(2)}) collective-permute-start(bf16[64,1792]{1,0:T(8,128)(2,1)} %get-tuple-element.19), channel_id=1, source_target_pairs={{0,8},{8,16},{16,24},{24,28},{28,20},{20,12},{12,4},{4,0},{1,9},{9... | collective-permute-start | bytes 688136 | tf_op jit(solution)/shard_map/ppermute | solution.py:81
  7.4 2.0 collective-permute-start
  13.3 6.4 %all-to-all-start.1 = ((bf16[8,1,128,736]{2,3,1,0:T(8,128)(2,1)}), bf16[8,1,128,736]{2,3,1,0:T(8,128)(2,1)S(1)}, u32[]{:S(2)}, u32[]{:S(2)}) async-start(bf16[8,1,128,736]{2,3,1,0:T(8,128)(2,1)} %pad_maximum_fusion.1), calls=%async_computation.1 | async-start | bytes 3014656 | tf_op jit(solution)/shard_map/all_to_all | solution.py:33
  48.5 2.1 broadcast.99.clone.1
  51.3 2.0 broadcast.99.clone
  63.6 2.1 collective-permute-start.18
  65.7 2.0 collective-permute-start.2
  74.4 1.9 collective-permute-start.20
  82.9 1.9 collective-permute-start.22
  84.9 2.9 %collective-permute-done.4 = bf16[64,1792]{1,0:T(8,128)(2,1)S(1)} collective-permute-done((bf16[64,1792]{1,0:T(8,128)(2,1)S(1)}, bf16[64,1792]{1,0:T(8,128)(2,1)S(1)}, u32[]{:S(2)}, u32[]{:S(2)}) %collective-permute-start.4) | collective-permute-done | bytes 229408 | tf_op jit(solution)/shard_map/ppermute | solution.py:81
  87.8 1.9 collective-permute-start.6
  92.7 1.9 collective-permute-start.24
  94.7 2.9 %collective-permute-done.6 = bf16[64,1792]{1,0:T(8,128)(2,1)S(1)} collective-permute-done((bf16[64,1792]{1,0:T(8,128)(2,1)S(1)}, bf16[64,1792]{1,0:T(8,128)(2,1)S(1)}, u32[]{:S(2)}, u32[]{:S(2)}) %collective-permute-start.6) | collective-permute-done | bytes 229408 | tf_op jit(solution)/shard_map/ppermute | solution.py:81
  97.6 1.9 collective-permute-start.8
  102.5 1.9 collective-permute-start.26
  104.6 2.8 %collective-permute-done.8 = bf16[64,1792]{1,0:T(8,128)(2,1)S(1)} collective-permute-done((bf16[64,1792]{1,0:T(8,128)(2,1)S(1)}, bf16[64,1792]{1,0:T(8,128)(2,1)S(1)}, u32[]{:S(2)}, u32[]{:S(2)}) %collective-permute-start.8) | collective-permute-done | bytes 229408 | tf_op jit(solution)/shard_map/ppermute | solution.py:81
  107.4 1.9 collective-permute-start.10
  112.4 1.9 collective-permute-start.28
  114.4 2.8 %collective-permute-done.10 = bf16[64,1792]{1,0:T(8,128)(2,1)S(1)} collective-permute-done((bf16[64,1792]{1,0:T(8,128)(2,1)S(1)}, bf16[64,1792]{1,0:T(8,128)(2,1)S(1)}, u32[]{:S(2)}, u32[]{:S(2)}) %collective-permute-start.10) | collective-permute-done | bytes 229408 | tf_op jit(solution)/shard_map/ppermute | solution.py:81
  117.3 1.9 collective-permute-start.12
  122.1 3.5 %collective-permute-done.12 = bf16[64,1792]{1,0:T(8,128)(2,1)S(1)} collective-permute-done((bf16[64,1792]{1,0:T(8,128)(2,1)S(1)}, bf16[64,1792]{1,0:T(8,128)(2,1)S(1)}, u32[]{:S(2)}, u32[]{:S(2)}) %collective-permute-start.12) | collective-permute-done | bytes 229408 | tf_op jit(solution)/shard_map/ppermute | solution.py:81
  127.8 3.3 %fusion.41 = f32[128,1024]{1,0:T(8,128)S(1)} fusion(bf16[128,1792]{1,0:T(8,128)(2,1)S(1)} %convolution_convert_fusion.4, bf16[1024,1792]{1,0:T(8,128)(2,1)} %bitcast.47), kind=kOutput, calls=%fused_computation.105 | convolution fusion | flops 469762048 | bytes 4653056 | tf_op jit(solution)/shard_map/dot_general | solution.py:136
  133.4 3.0 %fusion = bf16[128,1792]{1,0:T(8,128)(2,1)S(1)} fusion(bf16[128,1024]{1,0:T(8,128)(2,1)S(1)} %multiply_convert_fusion.2, bf16[1024,1792]{1,0:T(8,128)(2,1)} %bitcast.65, pred[]{:T(512)S(6)} %eq.61, bf16[1,128,3584]{2,1,0:T(8,128)(2,1)} %param.15, s32[]{:T(128)S(6)} %select_n.421, s32[128]{0:T(128)S(1)} %fusion.34), kind=kOutput, calls=%fused_computation.4 | convolution fusion | flops 529645568 | bytes 4850181 | tf_op jit(solution)/shard_map/dot_general | solution.py:145
  137.7 13.2 %collective-permute-done.30 = bf16[128,1792]{1,0:T(8,128)(2,1)} collective-permute-done((bf16[128,1792]{1,0:T(8,128)(2,1)S(1)}, bf16[128,1792]{1,0:T(8,128)(2,1)}, u32[]{:S(2)}, u32[]{:S(2)}) %collective-permute-start.30) | collective-permute-done | bytes 458784 | tf_op jit(solution)/shard_map/ppermute | solution.py:20
  151.0 2.3 select_select_fusion
  153.3 3.3 %fusion.42 = f32[128,1024]{1,0:T(8,128)S(1)} fusion(bf16[128,1792]{1,0:T(8,128)(2,1)S(1)} %get-tuple-element.37, bf16[1024,1792]{1,0:T(8,128)(2,1)} %bitcast.47), kind=kOutput, calls=%fused_computation.106 | convolution fusion | flops 469762048 | bytes 4653056 | tf_op jit(solution)/shard_map/dot_general | solution.py:136
  162.3 4.9 %all-to-all-start = ((bf16[8,1,128,736]{2,3,1,0:T(8,128)(2,1)}), bf16[8,1,128,736]{2,3,1,0:T(8,128)(2,1)S(1)}, u32[]{:S(2)}, u32[]{:S(2)}) async-start(bf16[8,1,128,736]{2,3,1,0:T(8,128)(2,1)} %pad_maximum_fusion), calls=%async_computation | async-start | bytes 3014656 | tf_op jit(solution)/shard_map/all_to_all | solution.py:33
  168.9 34.2 %all-to-all-done = bf16[8,1,128,736]{2,3,1,0:T(8,128)(2,1)S(1)} async-done(((bf16[8,1,128,736]{2,3,1,0:T(8,128)(2,1)}), bf16[8,1,128,736]{2,3,1,0:T(8,128)(2,1)S(1)}, u32[]{:S(2)}, u32[]{:S(2)}) %all-to-all-start) | async-done | bytes 1507360 | tf_op jit(solution)/shard_map/all_to_all | solution.py:33
  204.3 2.3 maximum_select_fusion.1
  209.8 3.6 %all-to-all-start.2 = ((bf16[8,128,448]{1,2,0:T(8,128)(2,1)}), bf16[8,128,448]{1,2,0:T(8,128)(2,1)S(1)}, u32[]{:S(2)}, u32[]{:S(2)}) async-start(bf16[8,128,448]{1,2,0:T(8,128)(2,1)} %pad_maximum_fusion.2), calls=%async_computation.2 | async-start | bytes 1835008 | tf_op jit(solution)/shard_map/all_to_all | solution.py:33
  213.4 3.9 %fusion.3 = bf16[1,128,1792]{2,1,0:T(8,128)(2,1)} fusion(bf16[128,1024]{1,0:T(8,128)(2,1)S(1)} %copy-done.7, bf16[1024,1792]{1,0:T(8,128)(2,1)} %bitcast.65, bf16[128,1792]{1,0:T(8,128)(2,1)S(1)} %copy-done.5, pred[]{:T(512)S(6)} %and.161, pred[]{:T(512)S(6)} %and.131, bf16[128,1792]{1,0:T(8,128)(2,1)} %collective-permute-done.30, ...), kind=kOutput, calls=%fused_computation.10 | convolution fusion | flops 530104320 | bytes 5767687 | tf_op jit(solution)/shard_map/dot_general | solution.py:145
  217.3 19.2 %all-to-all-done.2 = bf16[8,128,448]{1,2,0:T(8,128)(2,1)S(1)} async-done(((bf16[8,128,448]{1,2,0:T(8,128)(2,1)}), bf16[8,128,448]{1,2,0:T(8,128)(2,1)S(1)}, u32[]{:S(2)}, u32[]{:S(2)}) %all-to-all-start.2) | async-done | bytes 917536 | tf_op jit(solution)/shard_map/all_to_all | solution.py:33
  (140 shorter events, 56.6 us)
Async XLA Ops:
  2.5 61.0 %collective-permute-start.16 = (bf16[64,1792]{1,0:T(8,128)(2,1)}, bf16[64,1792]{1,0:T(8,128)(2,1)}, u32[]{:S(2)}, u32[]{:S(2)}) collective-permute-start(bf16[64,1792]{1,0:T(8,128)(2,1)} %get-tuple-element.19), channel_id=1, source_target_pairs={{0,8},{8,16},{16,24},{24,28},{28,20},{20,12},{12,4},{4,0},{1,9},{9... | collective-permute-start | bytes 688136 | tf_op jit(solution)/shard_map/ppermute | solution.py:81
  5.6 60.1 %collective-permute-start.17 = (bf16[64,1792]{1,0:T(8,128)(2,1)}, bf16[64,1792]{1,0:T(8,128)(2,1)}, u32[]{:S(2)}, u32[]{:S(2)}) collective-permute-start(bf16[64,1792]{1,0:T(8,128)(2,1)} %get-tuple-element.18), channel_id=1, source_target_pairs={{8,0},{16,8},{24,16},{28,24},{20,28},{12,20},{4,12},{0,4},{9,1},{1... | collective-permute-start | bytes 688136 | tf_op jit(solution)/shard_map/ppermute | solution.py:82
  7.4 58.3 %collective-permute-start = (bf16[64,1792]{1,0:T(8,128)(2,1)}, bf16[64,1792]{1,0:T(8,128)(2,1)}, u32[]{:S(2)}, u32[]{:S(2)}) collective-permute-start(bf16[64,1792]{1,0:T(8,128)(2,1)} %get-tuple-element.21), channel_id=1, source_target_pairs={{0,8},{8,16},{16,24},{24,28},{28,20},{20,12},{12,4},{4,0},{1,9},{9... | collective-permute-start | bytes 688136 | tf_op jit(solution)/shard_map/ppermute | solution.py:81
  9.5 61.5 %collective-permute-start.1 = (bf16[64,1792]{1,0:T(8,128)(2,1)}, bf16[64,1792]{1,0:T(8,128)(2,1)}, u32[]{:S(2)}, u32[]{:S(2)}) collective-permute-start(bf16[64,1792]{1,0:T(8,128)(2,1)} %get-tuple-element.20), channel_id=1, source_target_pairs={{8,0},{16,8},{24,16},{28,24},{20,28},{12,20},{4,12},{0,4},{9,1},{1... | collective-permute-start | bytes 688136 | tf_op jit(solution)/shard_map/ppermute | solution.py:82
  9.5 123.2 %collective-permute-start.15 = (bf16[1,128,512]{2,1,0:T(8,128)(2,1)}, bf16[1,128,512]{2,1,0:T(8,128)(2,1)S(1)}, u32[]{:S(2)}, u32[]{:S(2)}) collective-permute-start(bf16[1,128,512]{2,1,0:T(8,128)(2,1)} %param.14), channel_id=1, source_target_pairs={{0,1},{1,0},{2,3},{3,2},{4,5},{5,4},{6,7},{7,6},{8,9},{9,8},{10,11... | collective-permute-start | bytes 393224 | tf_op jit(solution)/shard_map/ppermute | solution.py:14
  13.3 148.9 %all-to-all-start.1 = ((bf16[8,1,128,736]{2,3,1,0:T(8,128)(2,1)}), bf16[8,1,128,736]{2,3,1,0:T(8,128)(2,1)S(1)}, u32[]{:S(2)}, u32[]{:S(2)}) async-start(bf16[8,1,128,736]{2,3,1,0:T(8,128)(2,1)} %pad_maximum_fusion.1), calls=%async_computation.1 | async-start | bytes 3014656 | tf_op jit(solution)/shard_map/all_to_all | solution.py:33
  63.6 10.8 %collective-permute-start.18 = (bf16[64,1792]{1,0:T(8,128)(2,1)}, bf16[64,1792]{1,0:T(8,128)(2,1)S(1)}, u32[]{:S(2)}, u32[]{:S(2)}) collective-permute-start(bf16[64,1792]{1,0:T(8,128)(2,1)} %collective-permute-done.16), channel_id=1, source_target_pairs={{0,8},{8,16},{16,24},{24,28},{28,20},{20,12},{12,4},{4,0},{1,9},{9... | collective-permute-start | bytes 688136 | tf_op jit(solution)/shard_map/ppermute | solution.py:81
  65.7 10.6 %collective-permute-start.19 = (bf16[64,1792]{1,0:T(8,128)(2,1)}, bf16[64,1792]{1,0:T(8,128)(2,1)S(1)}, u32[]{:S(2)}, u32[]{:S(2)}) collective-permute-start(bf16[64,1792]{1,0:T(8,128)(2,1)} %collective-permute-done.17), channel_id=1, source_target_pairs={{8,0},{16,8},{24,16},{28,24},{20,28},{12,20},{4,12},{0,4},{9,1},{1... | collective-permute-start | bytes 688136 | tf_op jit(solution)/shard_map/ppermute | solution.py:82
  65.7 11.2 %collective-permute-start.2 = (bf16[64,1792]{1,0:T(8,128)(2,1)}, bf16[64,1792]{1,0:T(8,128)(2,1)S(1)}, u32[]{:S(2)}, u32[]{:S(2)}) collective-permute-start(bf16[64,1792]{1,0:T(8,128)(2,1)} %collective-permute-done), channel_id=1, source_target_pairs={{0,8},{8,16},{16,24},{24,28},{28,20},{20,12},{12,4},{4,0},{1,9},{9... | collective-permute-start | bytes 688136 | tf_op jit(solution)/shard_map/ppermute | solution.py:81
  71.0 9.2 %collective-permute-start.3 = (bf16[64,1792]{1,0:T(8,128)(2,1)}, bf16[64,1792]{1,0:T(8,128)(2,1)S(1)}, u32[]{:S(2)}, u32[]{:S(2)}) collective-permute-start(bf16[64,1792]{1,0:T(8,128)(2,1)} %collective-permute-done.1), channel_id=1, source_target_pairs={{8,0},{16,8},{24,16},{28,24},{20,28},{12,20},{4,12},{0,4},{9,1},{1... | collective-permute-start | bytes 688136 | tf_op jit(solution)/shard_map/ppermute | solution.py:82
  74.4 8.5 %collective-permute-start.20 = (bf16[64,1792]{1,0:T(8,128)(2,1)S(1)}, bf16[64,1792]{1,0:T(8,128)(2,1)S(1)}, u32[]{:S(2)}, u32[]{:S(2)}) collective-permute-start(bf16[64,1792]{1,0:T(8,128)(2,1)S(1)} %collective-permute-done.18), channel_id=1, source_target_pairs={{0,8},{8,16},{16,24},{24,28},{28,20},{20,12},{12,4},{4,0},{1,9},{9... | collective-permute-start | bytes 688136 | tf_op jit(solution)/shard_map/ppermute | solution.py:81
  76.3 8.5 %collective-permute-start.21 = (bf16[64,1792]{1,0:T(8,128)(2,1)S(1)}, bf16[64,1792]{1,0:T(8,128)(2,1)S(1)}, u32[]{:S(2)}, u32[]{:S(2)}) collective-permute-start(bf16[64,1792]{1,0:T(8,128)(2,1)S(1)} %collective-permute-done.19), channel_id=1, source_target_pairs={{8,0},{16,8},{24,16},{28,24},{20,28},{12,20},{4,12},{0,4},{9,1},{1... | collective-permute-start | bytes 688136 | tf_op jit(solution)/shard_map/ppermute | solution.py:82
  76.9 10.9 %collective-permute-start.4 = (bf16[64,1792]{1,0:T(8,128)(2,1)S(1)}, bf16[64,1792]{1,0:T(8,128)(2,1)S(1)}, u32[]{:S(2)}, u32[]{:S(2)}) collective-permute-start(bf16[64,1792]{1,0:T(8,128)(2,1)S(1)} %collective-permute-done.2), channel_id=1, source_target_pairs={{0,8},{8,16},{16,24},{24,28},{28,20},{20,12},{12,4},{4,0},{1,9},{9... | collective-permute-start | bytes 688136 | tf_op jit(solution)/shard_map/ppermute | solution.py:81
  80.2 10.9 %collective-permute-start.5 = (bf16[64,1792]{1,0:T(8,128)(2,1)S(1)}, bf16[64,1792]{1,0:T(8,128)(2,1)S(1)}, u32[]{:S(2)}, u32[]{:S(2)}) collective-permute-start(bf16[64,1792]{1,0:T(8,128)(2,1)S(1)} %collective-permute-done.3), channel_id=1, source_target_pairs={{8,0},{16,8},{24,16},{28,24},{20,28},{12,20},{4,12},{0,4},{9,1},{1... | collective-permute-start | bytes 688136 | tf_op jit(solution)/shard_map/ppermute | solution.py:82
  82.9 9.8 %collective-permute-start.22 = (bf16[64,1792]{1,0:T(8,128)(2,1)S(1)}, bf16[64,1792]{1,0:T(8,128)(2,1)S(1)}, u32[]{:S(2)}, u32[]{:S(2)}) collective-permute-start(bf16[64,1792]{1,0:T(8,128)(2,1)S(1)} %collective-permute-done.20), channel_id=1, source_target_pairs={{0,8},{8,16},{16,24},{24,28},{28,20},{20,12},{12,4},{4,0},{1,9},{9... | collective-permute-start | bytes 688136 | tf_op jit(solution)/shard_map/ppermute | solution.py:81
  84.8 9.8 %collective-permute-start.23 = (bf16[64,1792]{1,0:T(8,128)(2,1)S(1)}, bf16[64,1792]{1,0:T(8,128)(2,1)S(1)}, u32[]{:S(2)}, u32[]{:S(2)}) collective-permute-start(bf16[64,1792]{1,0:T(8,128)(2,1)S(1)} %collective-permute-done.21), channel_id=1, source_target_pairs={{8,0},{16,8},{24,16},{28,24},{20,28},{12,20},{4,12},{0,4},{9,1},{1... | collective-permute-start | bytes 688136 | tf_op jit(solution)/shard_map/ppermute | solution.py:82
  87.8 9.8 %collective-permute-start.6 = (bf16[64,1792]{1,0:T(8,128)(2,1)S(1)}, bf16[64,1792]{1,0:T(8,128)(2,1)S(1)}, u32[]{:S(2)}, u32[]{:S(2)}) collective-permute-start(bf16[64,1792]{1,0:T(8,128)(2,1)S(1)} %collective-permute-done.4), channel_id=1, source_target_pairs={{0,8},{8,16},{16,24},{24,28},{28,20},{20,12},{12,4},{4,0},{1,9},{9... | collective-permute-start | bytes 688136 | tf_op jit(solution)/shard_map/ppermute | solution.py:81
  91.1 9.8 %collective-permute-start.7 = (bf16[64,1792]{1,0:T(8,128)(2,1)S(1)}, bf16[64,1792]{1,0:T(8,128)(2,1)S(1)}, u32[]{:S(2)}, u32[]{:S(2)}) collective-permute-start(bf16[64,1792]{1,0:T(8,128)(2,1)S(1)} %collective-permute-done.5), channel_id=1, source_target_pairs={{8,0},{16,8},{24,16},{28,24},{20,28},{12,20},{4,12},{0,4},{9,1},{1... | collective-permute-start | bytes 688136 | tf_op jit(solution)/shard_map/ppermute | solution.py:82
  92.7 9.8 %collective-permute-start.24 = (bf16[64,1792]{1,0:T(8,128)(2,1)S(1)}, bf16[64,1792]{1,0:T(8,128)(2,1)S(1)}, u32[]{:S(2)}, u32[]{:S(2)}) collective-permute-start(bf16[64,1792]{1,0:T(8,128)(2,1)S(1)} %collective-permute-done.22), channel_id=1, source_target_pairs={{0,8},{8,16},{16,24},{24,28},{28,20},{20,12},{12,4},{4,0},{1,9},{9... | collective-permute-start | bytes 688136 | tf_op jit(solution)/shard_map/ppermute | solution.py:81
  94.6 9.9 %collective-permute-start.25 = (bf16[64,1792]{1,0:T(8,128)(2,1)S(1)}, bf16[64,1792]{1,0:T(8,128)(2,1)S(1)}, u32[]{:S(2)}, u32[]{:S(2)}) collective-permute-start(bf16[64,1792]{1,0:T(8,128)(2,1)S(1)} %collective-permute-done.23), channel_id=1, source_target_pairs={{8,0},{16,8},{24,16},{28,24},{20,28},{12,20},{4,12},{0,4},{9,1},{1... | collective-permute-start | bytes 688136 | tf_op jit(solution)/shard_map/ppermute | solution.py:82
  97.6 9.8 %collective-permute-start.8 = (bf16[64,1792]{1,0:T(8,128)(2,1)S(1)}, bf16[64,1792]{1,0:T(8,128)(2,1)S(1)}, u32[]{:S(2)}, u32[]{:S(2)}) collective-permute-start(bf16[64,1792]{1,0:T(8,128)(2,1)S(1)} %collective-permute-done.6), channel_id=1, source_target_pairs={{0,8},{8,16},{16,24},{24,28},{28,20},{20,12},{12,4},{4,0},{1,9},{9... | collective-permute-start | bytes 688136 | tf_op jit(solution)/shard_map/ppermute | solution.py:81
  100.9 9.8 %collective-permute-start.9 = (bf16[64,1792]{1,0:T(8,128)(2,1)S(1)}, bf16[64,1792]{1,0:T(8,128)(2,1)S(1)}, u32[]{:S(2)}, u32[]{:S(2)}) collective-permute-start(bf16[64,1792]{1,0:T(8,128)(2,1)S(1)} %collective-permute-done.7), channel_id=1, source_target_pairs={{8,0},{16,8},{24,16},{28,24},{20,28},{12,20},{4,12},{0,4},{9,1},{1... | collective-permute-start | bytes 688136 | tf_op jit(solution)/shard_map/ppermute | solution.py:82
  102.5 9.8 %collective-permute-start.26 = (bf16[64,1792]{1,0:T(8,128)(2,1)S(1)}, bf16[64,1792]{1,0:T(8,128)(2,1)S(1)}, u32[]{:S(2)}, u32[]{:S(2)}) collective-permute-start(bf16[64,1792]{1,0:T(8,128)(2,1)S(1)} %collective-permute-done.24), channel_id=1, source_target_pairs={{0,8},{8,16},{16,24},{24,28},{28,20},{20,12},{12,4},{4,0},{1,9},{9... | collective-permute-start | bytes 688136 | tf_op jit(solution)/shard_map/ppermute | solution.py:81
  104.5 9.8 %collective-permute-start.27 = (bf16[64,1792]{1,0:T(8,128)(2,1)S(1)}, bf16[64,1792]{1,0:T(8,128)(2,1)S(1)}, u32[]{:S(2)}, u32[]{:S(2)}) collective-permute-start(bf16[64,1792]{1,0:T(8,128)(2,1)S(1)} %collective-permute-done.25), channel_id=1, source_target_pairs={{8,0},{16,8},{24,16},{28,24},{20,28},{12,20},{4,12},{0,4},{9,1},{1... | collective-permute-start | bytes 688136 | tf_op jit(solution)/shard_map/ppermute | solution.py:82
  107.4 9.8 %collective-permute-start.10 = (bf16[64,1792]{1,0:T(8,128)(2,1)S(1)}, bf16[64,1792]{1,0:T(8,128)(2,1)S(1)}, u32[]{:S(2)}, u32[]{:S(2)}) collective-permute-start(bf16[64,1792]{1,0:T(8,128)(2,1)S(1)} %collective-permute-done.8), channel_id=1, source_target_pairs={{0,8},{8,16},{16,24},{24,28},{28,20},{20,12},{12,4},{4,0},{1,9},{9... | collective-permute-start | bytes 688136 | tf_op jit(solution)/shard_map/ppermute | solution.py:81
  110.8 9.8 %collective-permute-start.11 = (bf16[64,1792]{1,0:T(8,128)(2,1)S(1)}, bf16[64,1792]{1,0:T(8,128)(2,1)S(1)}, u32[]{:S(2)}, u32[]{:S(2)}) collective-permute-start(bf16[64,1792]{1,0:T(8,128)(2,1)S(1)} %collective-permute-done.9), channel_id=1, source_target_pairs={{8,0},{16,8},{24,16},{28,24},{20,28},{12,20},{4,12},{0,4},{9,1},{1... | collective-permute-start | bytes 688136 | tf_op jit(solution)/shard_map/ppermute | solution.py:82
  112.4 18.9 %collective-permute-start.28 = (bf16[64,1792]{1,0:T(8,128)(2,1)S(1)}, bf16[64,1792]{1,0:T(8,128)(2,1)S(1)}, u32[]{:S(2)}, u32[]{:S(2)}) collective-permute-start(bf16[64,1792]{1,0:T(8,128)(2,1)S(1)} %collective-permute-done.26), channel_id=1, source_target_pairs={{0,8},{8,16},{16,24},{24,28},{28,20},{20,12},{12,4},{4,0},{1,9},{9... | collective-permute-start | bytes 688136 | tf_op jit(solution)/shard_map/ppermute | solution.py:81
  114.3 17.7 %collective-permute-start.29 = (bf16[64,1792]{1,0:T(8,128)(2,1)S(1)}, bf16[64,1792]{1,0:T(8,128)(2,1)S(1)}, u32[]{:S(2)}, u32[]{:S(2)}) collective-permute-start(bf16[64,1792]{1,0:T(8,128)(2,1)S(1)} %collective-permute-done.27), channel_id=1, source_target_pairs={{8,0},{16,8},{24,16},{28,24},{20,28},{12,20},{4,12},{0,4},{9,1},{1... | collective-permute-start | bytes 688136 | tf_op jit(solution)/shard_map/ppermute | solution.py:82
  136.4 14.6 %collective-permute-start.30 = (bf16[128,1792]{1,0:T(8,128)(2,1)S(1)}, bf16[128,1792]{1,0:T(8,128)(2,1)}, u32[]{:S(2)}, u32[]{:S(2)}) collective-permute-start(bf16[128,1792]{1,0:T(8,128)(2,1)S(1)} %fusion), channel_id=1, source_target_pairs={{2,0},{3,1},{6,4},{7,5},{10,8},{11,9},{14,12},{15,13},{18,16},{19,... | collective-permute-start | bytes 1376264 | tf_op jit(solution)/shard_map/ppermute | solution.py:20
  162.3 40.8 %all-to-all-start = ((bf16[8,1,128,736]{2,3,1,0:T(8,128)(2,1)}), bf16[8,1,128,736]{2,3,1,0:T(8,128)(2,1)S(1)}, u32[]{:S(2)}, u32[]{:S(2)}) async-start(bf16[8,1,128,736]{2,3,1,0:T(8,128)(2,1)} %pad_maximum_fusion), calls=%async_computation | async-start | bytes 3014656 | tf_op jit(solution)/shard_map/all_to_all | solution.py:33
  168.9 34.7 %collective-permute-start.33 = (bf16[8,1,128,512]{2,3,0,1:T(8,128)(2,1)}, bf16[8,1,128,512]{2,3,0,1:T(8,128)(2,1)}, u32[]{:S(2)}, u32[]{:S(2)}) collective-permute-start(bf16[8,1,128,512]{2,3,0,1:T(8,128)(2,1)} %get-tuple-element.17), channel_id=1, source_target_pairs={{0,1},{1,0},{2,3},{3,2},{4,5},{5,4},{6,7},{7,6},{8,9},{9,8},{10,11... | collective-permute-start | bytes 3145736 | tf_op jit(solution)/shard_map/ppermute | solution.py:14
  209.8 26.8 %all-to-all-start.2 = ((bf16[8,128,448]{1,2,0:T(8,128)(2,1)}), bf16[8,128,448]{1,2,0:T(8,128)(2,1)S(1)}, u32[]{:S(2)}, u32[]{:S(2)}) async-start(bf16[8,128,448]{1,2,0:T(8,128)(2,1)} %pad_maximum_fusion.2), calls=%async_computation.2 | async-start | bytes 1835008 | tf_op jit(solution)/shard_map/all_to_all | solution.py:33
  (20 other events, 244.0 us)

commit v2 on v1

--- a/solution.py
+++ b/solution.py
@@ -65,15 +65,15 @@
 def ring_gather(shard):
     count = lax.axis_size("dp")
     order = ring_order(count)
-    place = [0] * count
+    table = [None] * count
     for position, index in enumerate(order):
-        place[index] = position
-    here = jnp.asarray(place)[lax.axis_index("dp")]
-    order_table = jnp.asarray(order)
+        table[index] = [order[(position + step) % count] for step in range(count)]
+    owners = lax.dynamic_index_in_dim(
+        jnp.asarray(table, jnp.int32), lax.axis_index("dp"), 0, keepdims=False
+    )
     rows = shard.shape[0]
     half = rows // 2
-    out = jnp.zeros((count, rows) + shard.shape[1:], shard.dtype)
-    out = lax.dynamic_update_slice(out, shard[None], (lax.axis_index("dp"), 0, 0))
+    out = to_every(shard)
     ahead, behind = shard[:half], shard[half:]
     forth = [(order[k], order[(k + 1) % count]) for k in range(count)]
     back = [(high, low) for low, high in forth]
@@ -81,10 +81,10 @@
         ahead = lax.ppermute(ahead, "dp", forth)
         behind = lax.ppermute(behind, "dp", back)
         out = lax.dynamic_update_slice(
-            out, ahead[None], (order_table[(here - step) % count], 0, 0)
+            out, ahead[None], (owners[count - step], 0, 0)
         )
         out = lax.dynamic_update_slice(
-            out, behind[None], (order_table[(here + step) % count], half, 0)
+            out, behind[None], (owners[step], half, 0)
         )
     return out.reshape((count * rows,) + shard.shape[1:])
 
@@ -113,9 +113,14 @@
     slot_inputs = jnp.einsum(
         "mst,mtd->msd", onehot_all, layer_input, preferred_element_type=jnp.float32
     ).astype(jnp.bfloat16)
-    early = blocks_to_owners(
-        jnp.concatenate([to_every(hidden_here), column_blocks(slot_inputs)], -1)
+    early_blocks, up_half, down_half = lax.optimization_barrier(
+        (
+            jnp.concatenate([to_every(hidden_here), column_blocks(slot_inputs)], -1),
+            up_half,
+            down_half,
+        )
     )
+    early = blocks_to_owners(early_blocks)
     hidden_every = both_halves(early[..., :pre_width], core_index)
     top_half = lax.dynamic_slice_in_dim(top_grad, core_index * half_width, half_width, 2)
     tick_count = micro_count + layer_count - 1

time: 241 us -> 209 us (0.87)
  local copies, waits for them, and re-layouts: 43.1 us -> 19.2 us
  between operations: 37.4 us -> 14.5 us
  waiting for transfers between devices: 85.6 us -> 105 us
    dynamic_update_slice x30 -> x28, local copies, waits for them, and re-layouts: 25.1 us -> 4.31 us  [the longest x14 2.16 us: ring_gather(): lax.dynamic_update_slice(out, ahead[None], (owners[count - step], 0, 0))]
    ppermute x14, waiting for transfers between devices: 16.8 us -> 29.5 us  [ring_gather(): ahead = lax.ppermute(ahead, 'dp', forth)]
    all_to_all x3, waiting for transfers between devices: 53.4 us -> 59.1 us  [blocks_to_owners(): return lax.all_to_all(blocks, 'dp', 0, 0, tiled=True)]
    another operation x3 -> x1, local copies, waits for them, and re-layouts: 4.22 us -> 0.12 us
    all_to_all x3, starting transfers between devices: 15 us -> 12.2 us  [blocks_to_owners(): return lax.all_to_all(blocks, 'dp', 0, 0, tiled=True)]
  transfers between devices with their start and end apart: 37 -> 37, of which waited for: 18 -> 19; matrix products, arithmetic and copies ran while one was open for 26% -> 16% of each run, Pallas kernels for 0% -> 0%
where the time goes in v2:
time: 209 us; the launch traced here: 208 us
  waiting for transfers between devices  105 us (50%)
  starting transfers between devices  44 us (21%)
  local copies, waits for them, and re-layouts  19.2 us (9%)
  matrix products  16 us (8%)
  between operations  14.5 us (7%)
  other arithmetic  9.19 us (4%)
    all_to_all x3, waiting for transfers between devices, blocks_to_owners(): return lax.all_to_all(blocks, 'dp', 0, 0, tiled=True)  59.1 us
    ppermute x14, waiting for transfers between devices, ring_gather(): ahead = lax.ppermute(ahead, 'dp', forth)  29.5 us
    ppermute x14, starting transfers between devices, ring_gather(): ahead = lax.ppermute(ahead, 'dp', forth)  28.4 us
    ppermute x1, waiting for transfers between devices, passed_along(): return lax.ppermute(shard, axis, pairs)  12.8 us
    all_to_all x3, starting transfers between devices, blocks_to_owners(): return lax.all_to_all(blocks, 'dp', 0, 0, tiled=True)  12.2 us
    dot_general x2, matrix products, local(): lax.dot_general(onehot, slot_input_grad, (((0,), (0,)), ((), ())), prefer...  6.89 us
    dot_general x2, matrix products, local(): lax.dot_general(slot_grad, down_half, (((1,), (1,)), ((), ())), preferred...  4.62 us
    unnamed x32, local copies, waits for them, and re-layouts  4.41 us
  transfers between devices with their start and end apart: 37, of which 19 were waited for; matrix products, arithmetic and copies ran while one was open for 16% of the time, Pallas kernels for 0%

profile of v2, /device:TPU:0, one launch (start us, length us, event | category | flops | bytes accessed | tf_op | source)
XLA Modules:
  0.0 208.1 jit_solution(3422577718935059500)
XLA Ops:
  2.5 3.1 %collective-permute-start.14 = (bf16[64,1792]{1,0:T(8,128)(2,1)}, bf16[64,1792]{1,0:T(8,128)(2,1)}, u32[]{:S(2)}, u32[]{:S(2)}) collective-permute-start(bf16[64,1792]{1,0:T(8,128)(2,1)} %get-tuple-element.25), channel_id=1, source_target_pairs={{0,8},{8,16},{16,24},{24,28},{28,20},{20,12},{12,4},{4,0},{1,9},{9... | collective-permute-start | bytes 688136 | tf_op jit(solution)/shard_map/ppermute | solution.py:81
  27.4 2.0 collective-permute-start.16
  36.1 1.9 collective-permute-start.18
  38.1 2.9 %collective-permute-done.2 = bf16[64,1792]{1,0:T(8,128)(2,1)S(1)} collective-permute-done((bf16[64,1792]{1,0:T(8,128)(2,1)}, bf16[64,1792]{1,0:T(8,128)(2,1)S(1)}, u32[]{:S(2)}, u32[]{:S(2)}) %collective-permute-start.2) | collective-permute-done | bytes 229408 | tf_op jit(solution)/shard_map/ppermute | solution.py:81
  41.0 1.9 collective-permute-start.4
  43.2 2.7 %collective-permute-done.18 = bf16[64,1792]{1,0:T(8,128)(2,1)S(1)} collective-permute-done((bf16[64,1792]{1,0:T(8,128)(2,1)S(1)}, bf16[64,1792]{1,0:T(8,128)(2,1)S(1)}, u32[]{:S(2)}, u32[]{:S(2)}) %collective-permute-start.18) | collective-permute-done | bytes 229408 | tf_op jit(solution)/shard_map/ppermute | solution.py:81
  45.9 1.9 collective-permute-start.20
  48.0 2.9 %collective-permute-done.4 = bf16[64,1792]{1,0:T(8,128)(2,1)S(1)} collective-permute-done((bf16[64,1792]{1,0:T(8,128)(2,1)S(1)}, bf16[64,1792]{1,0:T(8,128)(2,1)S(1)}, u32[]{:S(2)}, u32[]{:S(2)}) %collective-permute-start.4) | collective-permute-done | bytes 229408 | tf_op jit(solution)/shard_map/ppermute | solution.py:81
  53.0 2.7 %collective-permute-done.20 = bf16[64,1792]{1,0:T(8,128)(2,1)S(1)} collective-permute-done((bf16[64,1792]{1,0:T(8,128)(2,1)S(1)}, bf16[64,1792]{1,0:T(8,128)(2,1)S(1)}, u32[]{:S(2)}, u32[]{:S(2)}) %collective-permute-start.20) | collective-permute-done | bytes 229408 | tf_op jit(solution)/shard_map/ppermute | solution.py:81
  55.8 1.9 collective-permute-start.22
  57.8 2.8 %collective-permute-done.6 = bf16[64,1792]{1,0:T(8,128)(2,1)S(1)} collective-permute-done((bf16[64,1792]{1,0:T(8,128)(2,1)S(1)}, bf16[64,1792]{1,0:T(8,128)(2,1)S(1)}, u32[]{:S(2)}, u32[]{:S(2)}) %collective-permute-start.6) | collective-permute-done | bytes 229408 | tf_op jit(solution)/shard_map/ppermute | solution.py:81
  60.7 1.9 collective-permute-start.8
  62.8 2.8 %collective-permute-done.22 = bf16[64,1792]{1,0:T(8,128)(2,1)S(1)} collective-permute-done((bf16[64,1792]{1,0:T(8,128)(2,1)S(1)}, bf16[64,1792]{1,0:T(8,128)(2,1)S(1)}, u32[]{:S(2)}, u32[]{:S(2)}) %collective-permute-start.22) | collective-permute-done | bytes 229408 | tf_op jit(solution)/shard_map/ppermute | solution.py:81
  65.6 1.9 collective-permute-start.24
  67.7 2.8 %collective-permute-done.8 = bf16[64,1792]{1,0:T(8,128)(2,1)S(1)} collective-permute-done((bf16[64,1792]{1,0:T(8,128)(2,1)S(1)}, bf16[64,1792]{1,0:T(8,128)(2,1)S(1)}, u32[]{:S(2)}, u32[]{:S(2)}) %collective-permute-start.8) | collective-permute-done | bytes 229408 | tf_op jit(solution)/shard_map/ppermute | solution.py:81
  70.5 1.9 collective-permute-start.10
  72.6 2.8 %collective-permute-done.24 = bf16[64,1792]{1,0:T(8,128)(2,1)S(1)} collective-permute-done((bf16[64,1792]{1,0:T(8,128)(2,1)S(1)}, bf16[64,1792]{1,0:T(8,128)(2,1)S(1)}, u32[]{:S(2)}, u32[]{:S(2)}) %collective-permute-start.24) | collective-permute-done | bytes 229408 | tf_op jit(solution)/shard_map/ppermute | solution.py:81
  77.6 2.8 %collective-permute-done.10 = bf16[64,1792]{1,0:T(8,128)(2,1)S(1)} collective-permute-done((bf16[64,1792]{1,0:T(8,128)(2,1)S(1)}, bf16[64,1792]{1,0:T(8,128)(2,1)S(1)}, u32[]{:S(2)}, u32[]{:S(2)}) %collective-permute-start.10) | collective-permute-done | bytes 229408 | tf_op jit(solution)/shard_map/ppermute | solution.py:81
  80.3 1.9 collective-permute-start.12
  82.5 2.8 %collective-permute-done.26 = bf16[64,1792]{1,0:T(8,128)(2,1)S(1)} collective-permute-done((bf16[64,1792]{1,0:T(8,128)(2,1)S(1)}, bf16[64,1792]{1,0:T(8,128)(2,1)S(1)}, u32[]{:S(2)}, u32[]{:S(2)}) %collective-permute-start.26) | collective-permute-done | bytes 229408 | tf_op jit(solution)/shard_map/ppermute | solution.py:81
  92.0 4.8 %all-to-all-start.1 = ((bf16[8,1,128,736]{2,3,1,0:T(8,128)(2,1)}), bf16[8,1,128,736]{2,3,1,0:T(8,128)(2,1)S(1)}, u32[]{:S(2)}, u32[]{:S(2)}) async-start(bf16[8,1,128,736]{2,3,1,0:T(8,128)(2,1)} %pad_maximum_fusion), calls=%async_computation.1 | async-start | bytes 3014656 | tf_op jit(solution)/shard_map/all_to_all | solution.py:33
  98.2 3.0 %fusion = bf16[128,1792]{1,0:T(8,128)(2,1)S(1)} fusion(bf16[128,1024]{1,0:T(8,128)(2,1)S(1)} %multiply_convert_fusion.2, bf16[1024,1792]{1,0:T(8,128)(2,1)} %bitcast.154, pred[]{:T(512)S(6)} %eq.33, bf16[1,128,3584]{2,1,0:T(8,128)(2,1)} %param.13, s32[]{:T(128)S(6)} %select_n.196, s32[128]{0:T(128)S(1)} %fusion.34), kind=kOutput, calls=%fused_computation.4 | convolution fusion | flops 529645568 | bytes 4850181 | tf_op jit(solution)/shard_map/dot_general | solution.py:150
  102.5 12.8 %collective-permute-done.30 = bf16[128,1792]{1,0:T(8,128)(2,1)} collective-permute-done((bf16[128,1792]{1,0:T(8,128)(2,1)S(1)}, bf16[128,1792]{1,0:T(8,128)(2,1)}, u32[]{:S(2)}, u32[]{:S(2)}) %collective-permute-start.30) | collective-permute-done | bytes 458784 | tf_op jit(solution)/shard_map/ppermute | solution.py:20
  115.3 2.3 %select_select_fusion = (bf16[128,1792]{1,0:T(8,128)(2,1)}, bf16[128,1792]{1,0:T(8,128)(2,1)S(1)}) fusion(bf16[128,1792]{1,0:T(8,128)(2,1)S(1)} %copy-done.13, pred[]{:T(512)S(6)} %and.21, pred[]{:T(512)S(6)} %and.19, f32[128]{0:T(128)S(1)} %fusion.35, bf16[128,1792]{1,0:T(8,128)(2,1)} %collective-permute-done.30, bf16[1,128,3584]{2,1,0:T(8,128)(2,1)} %param.13, ...), kind=kOutput, calls=%fused_computation.39 | convolution fusion | flops 60342272 | bytes 2294791 | tf_op jit(solution)/shard_map/dot_general | solution.py:140
  117.6 3.3 %fusion.42 = f32[128,1024]{1,0:T(8,128)S(1)} fusion(bf16[128,1792]{1,0:T(8,128)(2,1)S(1)} %get-tuple-element.36, bf16[1024,1792]{1,0:T(8,128)(2,1)} %bitcast.153), kind=kOutput, calls=%fused_computation.105 | convolution fusion | flops 469762048 | bytes 4653056 | tf_op jit(solution)/shard_map/dot_general | solution.py:141
  126.6 6.0 %all-to-all-done.1 = bf16[8,1,128,736]{2,3,1,0:T(8,128)(2,1)S(1)} async-done(((bf16[8,1,128,736]{2,3,1,0:T(8,128)(2,1)}), bf16[8,1,128,736]{2,3,1,0:T(8,128)(2,1)S(1)}, u32[]{:S(2)}, u32[]{:S(2)}) %all-to-all-start.1) | async-done | bytes 1507360 | tf_op jit(solution)/shard_map/all_to_all | solution.py:33
  132.6 3.8 %all-to-all-start = ((bf16[8,1,128,736]{2,3,1,0:T(8,128)(2,1)}), bf16[8,1,128,736]{2,3,1,0:T(8,128)(2,1)S(1)}, u32[]{:S(2)}, u32[]{:S(2)}) async-start(bf16[8,1,128,736]{2,3,1,0:T(8,128)(2,1)} %pad_maximum_fusion.1), calls=%async_computation | async-start | bytes 3014656 | tf_op jit(solution)/shard_map/all_to_all | solution.py:33
  138.1 34.0 %all-to-all-done = bf16[8,1,128,736]{2,3,1,0:T(8,128)(2,1)S(1)} async-done(((bf16[8,1,128,736]{2,3,1,0:T(8,128)(2,1)}), bf16[8,1,128,736]{2,3,1,0:T(8,128)(2,1)S(1)}, u32[]{:S(2)}, u32[]{:S(2)}) %all-to-all-start) | async-done | bytes 1507360 | tf_op jit(solution)/shard_map/all_to_all | solution.py:33
  173.3 2.2 %maximum_select_fusion.1 = bf16[8,128,1024]{1,2,0:T(8,128)(2,1)S(1)} fusion(bf16[8,128,512]{1,2,0:T(8,128)(2,1)} %bitcast.63, bf16[8,128,512]{1,2,0:T(8,128)(2,1)S(1)} %copy-done.3, pred[]{:T(512)S(6)} %eq.38), kind=kLoop, calls=%fused_computation.12 | loop fusion | flops 9437184 | bytes 4194305 | tf_op jit(solution)/shard_map/jit(_where)/select_n | solution.py:48
  178.6 3.6 %all-to-all-start.2 = ((bf16[8,128,448]{1,2,0:T(8,128)(2,1)}), bf16[8,128,448]{1,2,0:T(8,128)(2,1)S(1)}, u32[]{:S(2)}, u32[]{:S(2)}) async-start(bf16[8,128,448]{1,2,0:T(8,128)(2,1)} %pad_maximum_fusion.2), calls=%async_computation.2 | async-start | bytes 1835008 | tf_op jit(solution)/shard_map/all_to_all | solution.py:33
  182.3 3.9 %fusion.3 = bf16[1,128,1792]{2,1,0:T(8,128)(2,1)} fusion(bf16[128,1024]{1,0:T(8,128)(2,1)S(1)} %copy-done.9, bf16[1024,1792]{1,0:T(8,128)(2,1)} %bitcast.155, bf16[128,1792]{1,0:T(8,128)(2,1)S(1)} %copy-done.7, pred[]{:T(512)S(6)} %and.21, pred[]{:T(512)S(6)} %and.19, bf16[128,1792]{1,0:T(8,128)(2,1)} %collective-permute-done.30, ...), kind=kOutput, calls=%fused_computation.10 | convolution fusion | flops 530104320 | bytes 5767687 | tf_op jit(solution)/shard_map/dot_general | solution.py:150
  186.2 19.2 %all-to-all-done.2 = bf16[8,128,448]{1,2,0:T(8,128)(2,1)S(1)} async-done(((bf16[8,128,448]{1,2,0:T(8,128)(2,1)}), bf16[8,128,448]{1,2,0:T(8,128)(2,1)S(1)}, u32[]{:S(2)}, u32[]{:S(2)}) %all-to-all-start.2) | async-done | bytes 917536 | tf_op jit(solution)/shard_map/all_to_all | solution.py:33
  (138 shorter events, 46.2 us)
Async XLA Ops:
  2.5 24.9 %collective-permute-start.14 = (bf16[64,1792]{1,0:T(8,128)(2,1)}, bf16[64,1792]{1,0:T(8,128)(2,1)}, u32[]{:S(2)}, u32[]{:S(2)}) collective-permute-start(bf16[64,1792]{1,0:T(8,128)(2,1)} %get-tuple-element.25), channel_id=1, source_target_pairs={{0,8},{8,16},{16,24},{24,28},{28,20},{20,12},{12,4},{4,0},{1,9},{9... | collective-permute-start | bytes 688136 | tf_op jit(solution)/shard_map/ppermute | solution.py:81
  5.5 23.8 %collective-permute-start.15 = (bf16[64,1792]{1,0:T(8,128)(2,1)S(1)}, bf16[64,1792]{1,0:T(8,128)(2,1)}, u32[]{:S(2)}, u32[]{:S(2)}) collective-permute-start(bf16[64,1792]{1,0:T(8,128)(2,1)S(1)} %get-tuple-element.24), channel_id=1, source_target_pairs={{8,0},{16,8},{24,16},{28,24},{20,28},{12,20},{4,12},{0,4},{9,1},{1... | collective-permute-start | bytes 688136 | tf_op jit(solution)/shard_map/ppermute | solution.py:82
  7.4 22.1 %collective-permute-start = (bf16[64,1792]{1,0:T(8,128)(2,1)}, bf16[64,1792]{1,0:T(8,128)(2,1)}, u32[]{:S(2)}, u32[]{:S(2)}) collective-permute-start(bf16[64,1792]{1,0:T(8,128)(2,1)} %get-tuple-element.27), channel_id=1, source_target_pairs={{0,8},{8,16},{16,24},{24,28},{28,20},{20,12},{12,4},{4,0},{1,9},{9... | collective-permute-start | bytes 688136 | tf_op jit(solution)/shard_map/ppermute | solution.py:81
  9.3 24.5 %collective-permute-start.1 = (bf16[64,1792]{1,0:T(8,128)(2,1)S(1)}, bf16[64,1792]{1,0:T(8,128)(2,1)}, u32[]{:S(2)}, u32[]{:S(2)}) collective-permute-start(bf16[64,1792]{1,0:T(8,128)(2,1)S(1)} %get-tuple-element.26), channel_id=1, source_target_pairs={{8,0},{16,8},{24,16},{28,24},{20,28},{12,20},{4,12},{0,4},{9,1},{1... | collective-permute-start | bytes 688136 | tf_op jit(solution)/shard_map/ppermute | solution.py:82
  27.4 8.7 %collective-permute-start.16 = (bf16[64,1792]{1,0:T(8,128)(2,1)}, bf16[64,1792]{1,0:T(8,128)(2,1)S(1)}, u32[]{:S(2)}, u32[]{:S(2)}) collective-permute-start(bf16[64,1792]{1,0:T(8,128)(2,1)} %collective-permute-done.14), channel_id=1, source_target_pairs={{0,8},{8,16},{16,24},{24,28},{28,20},{20,12},{12,4},{4,0},{1,9},{9... | collective-permute-start | bytes 688136 | tf_op jit(solution)/shard_map/ppermute | solution.py:81
  29.4 8.7 %collective-permute-start.17 = (bf16[64,1792]{1,0:T(8,128)(2,1)}, bf16[64,1792]{1,0:T(8,128)(2,1)S(1)}, u32[]{:S(2)}, u32[]{:S(2)}) collective-permute-start(bf16[64,1792]{1,0:T(8,128)(2,1)} %collective-permute-done.15), channel_id=1, source_target_pairs={{8,0},{16,8},{24,16},{28,24},{20,28},{12,20},{4,12},{0,4},{9,1},{1... | collective-permute-start | bytes 688136 | tf_op jit(solution)/shard_map/ppermute | solution.py:82
  29.4 11.6 %collective-permute-start.2 = (bf16[64,1792]{1,0:T(8,128)(2,1)}, bf16[64,1792]{1,0:T(8,128)(2,1)S(1)}, u32[]{:S(2)}, u32[]{:S(2)}) collective-permute-start(bf16[64,1792]{1,0:T(8,128)(2,1)} %collective-permute-done), channel_id=1, source_target_pairs={{0,8},{8,16},{16,24},{24,28},{28,20},{20,12},{12,4},{4,0},{1,9},{9... | collective-permute-start | bytes 688136 | tf_op jit(solution)/shard_map/ppermute | solution.py:81
  33.9 9.2 %collective-permute-start.3 = (bf16[64,1792]{1,0:T(8,128)(2,1)}, bf16[64,1792]{1,0:T(8,128)(2,1)S(1)}, u32[]{:S(2)}, u32[]{:S(2)}) collective-permute-start(bf16[64,1792]{1,0:T(8,128)(2,1)} %collective-permute-done.1), channel_id=1, source_target_pairs={{8,0},{16,8},{24,16},{28,24},{20,28},{12,20},{4,12},{0,4},{9,1},{1... | collective-permute-start | bytes 688136 | tf_op jit(solution)/shard_map/ppermute | solution.py:82
  36.1 9.8 %collective-permute-start.18 = (bf16[64,1792]{1,0:T(8,128)(2,1)S(1)}, bf16[64,1792]{1,0:T(8,128)(2,1)S(1)}, u32[]{:S(2)}, u32[]{:S(2)}) collective-permute-start(bf16[64,1792]{1,0:T(8,128)(2,1)S(1)} %collective-permute-done.16), channel_id=1, source_target_pairs={{0,8},{8,16},{16,24},{24,28},{28,20},{20,12},{12,4},{4,0},{1,9},{9... | collective-permute-start | bytes 688136 | tf_op jit(solution)/shard_map/ppermute | solution.py:81
  38.0 9.8 %collective-permute-start.19 = (bf16[64,1792]{1,0:T(8,128)(2,1)S(1)}, bf16[64,1792]{1,0:T(8,128)(2,1)S(1)}, u32[]{:S(2)}, u32[]{:S(2)}) collective-permute-start(bf16[64,1792]{1,0:T(8,128)(2,1)S(1)} %collective-permute-done.17), channel_id=1, source_target_pairs={{8,0},{16,8},{24,16},{28,24},{20,28},{12,20},{4,12},{0,4},{9,1},{1... | collective-permute-start | bytes 688136 | tf_op jit(solution)/shard_map/ppermute | solution.py:82
  41.0 9.8 %collective-permute-start.4 = (bf16[64,1792]{1,0:T(8,128)(2,1)S(1)}, bf16[64,1792]{1,0:T(8,128)(2,1)S(1)}, u32[]{:S(2)}, u32[]{:S(2)}) collective-permute-start(bf16[64,1792]{1,0:T(8,128)(2,1)S(1)} %collective-permute-done.2), channel_id=1, source_target_pairs={{0,8},{8,16},{16,24},{24,28},{28,20},{20,12},{12,4},{4,0},{1,9},{9... | collective-permute-start | bytes 688136 | tf_op jit(solution)/shard_map/ppermute | solution.py:81
  43.0 9.8 %collective-permute-start.5 = (bf16[64,1792]{1,0:T(8,128)(2,1)S(1)}, bf16[64,1792]{1,0:T(8,128)(2,1)S(1)}, u32[]{:S(2)}, u32[]{:S(2)}) collective-permute-start(bf16[64,1792]{1,0:T(8,128)(2,1)S(1)} %collective-permute-done.3), channel_id=1, source_target_pairs={{8,0},{16,8},{24,16},{28,24},{20,28},{12,20},{4,12},{0,4},{9,1},{1... | collective-permute-start | bytes 688136 | tf_op jit(solution)/shard_map/ppermute | solution.py:82
  45.9 9.8 %collective-permute-start.20 = (bf16[64,1792]{1,0:T(8,128)(2,1)S(1)}, bf16[64,1792]{1,0:T(8,128)(2,1)S(1)}, u32[]{:S(2)}, u32[]{:S(2)}) collective-permute-start(bf16[64,1792]{1,0:T(8,128)(2,1)S(1)} %collective-permute-done.18), channel_id=1, source_target_pairs={{0,8},{8,16},{16,24},{24,28},{28,20},{20,12},{12,4},{4,0},{1,9},{9... | collective-permute-start | bytes 688136 | tf_op jit(solution)/shard_map/ppermute | solution.py:81
  47.9 9.8 %collective-permute-start.21 = (bf16[64,1792]{1,0:T(8,128)(2,1)S(1)}, bf16[64,1792]{1,0:T(8,128)(2,1)S(1)}, u32[]{:S(2)}, u32[]{:S(2)}) collective-permute-start(bf16[64,1792]{1,0:T(8,128)(2,1)S(1)} %collective-permute-done.19), channel_id=1, source_target_pairs={{8,0},{16,8},{24,16},{28,24},{20,28},{12,20},{4,12},{0,4},{9,1},{1... | collective-permute-start | bytes 688136 | tf_op jit(solution)/shard_map/ppermute | solution.py:82
  50.8 9.8 %collective-permute-start.6 = (bf16[64,1792]{1,0:T(8,128)(2,1)S(1)}, bf16[64,1792]{1,0:T(8,128)(2,1)S(1)}, u32[]{:S(2)}, u32[]{:S(2)}) collective-permute-start(bf16[64,1792]{1,0:T(8,128)(2,1)S(1)} %collective-permute-done.4), channel_id=1, source_target_pairs={{0,8},{8,16},{16,24},{24,28},{28,20},{20,12},{12,4},{4,0},{1,9},{9... | collective-permute-start | bytes 688136 | tf_op jit(solution)/shard_map/ppermute | solution.py:81
  52.9 9.8 %collective-permute-start.7 = (bf16[64,1792]{1,0:T(8,128)(2,1)S(1)}, bf16[64,1792]{1,0:T(8,128)(2,1)S(1)}, u32[]{:S(2)}, u32[]{:S(2)}) collective-permute-start(bf16[64,1792]{1,0:T(8,128)(2,1)S(1)} %collective-permute-done.5), channel_id=1, source_target_pairs={{8,0},{16,8},{24,16},{28,24},{20,28},{12,20},{4,12},{0,4},{9,1},{1... | collective-permute-start | bytes 688136 | tf_op jit(solution)/shard_map/ppermute | solution.py:82
  55.8 9.8 %collective-permute-start.22 = (bf16[64,1792]{1,0:T(8,128)(2,1)S(1)}, bf16[64,1792]{1,0:T(8,128)(2,1)S(1)}, u32[]{:S(2)}, u32[]{:S(2)}) collective-permute-start(bf16[64,1792]{1,0:T(8,128)(2,1)S(1)} %collective-permute-done.20), channel_id=1, source_target_pairs={{0,8},{8,16},{16,24},{24,28},{28,20},{20,12},{12,4},{4,0},{1,9},{9... | collective-permute-start | bytes 688136 | tf_op jit(solution)/shard_map/ppermute | solution.py:81
  57.7 9.9 %collective-permute-start.23 = (bf16[64,1792]{1,0:T(8,128)(2,1)S(1)}, bf16[64,1792]{1,0:T(8,128)(2,1)S(1)}, u32[]{:S(2)}, u32[]{:S(2)}) collective-permute-start(bf16[64,1792]{1,0:T(8,128)(2,1)S(1)} %collective-permute-done.21), channel_id=1, source_target_pairs={{8,0},{16,8},{24,16},{28,24},{20,28},{12,20},{4,12},{0,4},{9,1},{1... | collective-permute-start | bytes 688136 | tf_op jit(solution)/shard_map/ppermute | solution.py:82
  60.7 9.8 %collective-permute-start.8 = (bf16[64,1792]{1,0:T(8,128)(2,1)S(1)}, bf16[64,1792]{1,0:T(8,128)(2,1)S(1)}, u32[]{:S(2)}, u32[]{:S(2)}) collective-permute-start(bf16[64,1792]{1,0:T(8,128)(2,1)S(1)} %collective-permute-done.6), channel_id=1, source_target_pairs={{0,8},{8,16},{16,24},{24,28},{28,20},{20,12},{12,4},{4,0},{1,9},{9... | collective-permute-start | bytes 688136 | tf_op jit(solution)/shard_map/ppermute | solution.py:81
  62.7 9.8 %collective-permute-start.9 = (bf16[64,1792]{1,0:T(8,128)(2,1)S(1)}, bf16[64,1792]{1,0:T(8,128)(2,1)S(1)}, u32[]{:S(2)}, u32[]{:S(2)}) collective-permute-start(bf16[64,1792]{1,0:T(8,128)(2,1)S(1)} %collective-permute-done.7), channel_id=1, source_target_pairs={{8,0},{16,8},{24,16},{28,24},{20,28},{12,20},{4,12},{0,4},{9,1},{1... | collective-permute-start | bytes 688136 | tf_op jit(solution)/shard_map/ppermute | solution.py:82
  65.6 9.8 %collective-permute-start.24 = (bf16[64,1792]{1,0:T(8,128)(2,1)S(1)}, bf16[64,1792]{1,0:T(8,128)(2,1)S(1)}, u32[]{:S(2)}, u32[]{:S(2)}) collective-permute-start(bf16[64,1792]{1,0:T(8,128)(2,1)S(1)} %collective-permute-done.22), channel_id=1, source_target_pairs={{0,8},{8,16},{16,24},{24,28},{28,20},{20,12},{12,4},{4,0},{1,9},{9... | collective-permute-start | bytes 688136 | tf_op jit(solution)/shard_map/ppermute | solution.py:81
  67.6 9.8 %collective-permute-start.25 = (bf16[64,1792]{1,0:T(8,128)(2,1)S(1)}, bf16[64,1792]{1,0:T(8,128)(2,1)S(1)}, u32[]{:S(2)}, u32[]{:S(2)}) collective-permute-start(bf16[64,1792]{1,0:T(8,128)(2,1)S(1)} %collective-permute-done.23), channel_id=1, source_target_pairs={{8,0},{16,8},{24,16},{28,24},{20,28},{12,20},{4,12},{0,4},{9,1},{1... | collective-permute-start | bytes 688136 | tf_op jit(solution)/shard_map/ppermute | solution.py:82
  70.5 9.8 %collective-permute-start.10 = (bf16[64,1792]{1,0:T(8,128)(2,1)S(1)}, bf16[64,1792]{1,0:T(8,128)(2,1)S(1)}, u32[]{:S(2)}, u32[]{:S(2)}) collective-permute-start(bf16[64,1792]{1,0:T(8,128)(2,1)S(1)} %collective-permute-done.8), channel_id=1, source_target_pairs={{0,8},{8,16},{16,24},{24,28},{28,20},{20,12},{12,4},{4,0},{1,9},{9... | collective-permute-start | bytes 688136 | tf_op jit(solution)/shard_map/ppermute | solution.py:81
  72.5 9.8 %collective-permute-start.11 = (bf16[64,1792]{1,0:T(8,128)(2,1)S(1)}, bf16[64,1792]{1,0:T(8,128)(2,1)S(1)}, u32[]{:S(2)}, u32[]{:S(2)}) collective-permute-start(bf16[64,1792]{1,0:T(8,128)(2,1)S(1)} %collective-permute-done.9), channel_id=1, source_target_pairs={{8,0},{16,8},{24,16},{28,24},{20,28},{12,20},{4,12},{0,4},{9,1},{1... | collective-permute-start | bytes 688136 | tf_op jit(solution)/shard_map/ppermute | solution.py:82
  75.4 9.8 %collective-permute-start.26 = (bf16[64,1792]{1,0:T(8,128)(2,1)S(1)}, bf16[64,1792]{1,0:T(8,128)(2,1)S(1)}, u32[]{:S(2)}, u32[]{:S(2)}) collective-permute-start(bf16[64,1792]{1,0:T(8,128)(2,1)S(1)} %collective-permute-done.24), channel_id=1, source_target_pairs={{0,8},{8,16},{16,24},{24,28},{28,20},{20,12},{12,4},{4,0},{1,9},{9... | collective-permute-start | bytes 688136 | tf_op jit(solution)/shard_map/ppermute | solution.py:81
  77.4 9.4 %collective-permute-start.27 = (bf16[64,1792]{1,0:T(8,128)(2,1)S(1)}, bf16[64,1792]{1,0:T(8,128)(2,1)S(1)}, u32[]{:S(2)}, u32[]{:S(2)}) collective-permute-start(bf16[64,1792]{1,0:T(8,128)(2,1)S(1)} %collective-permute-done.25), channel_id=1, source_target_pairs={{8,0},{16,8},{24,16},{28,24},{20,28},{12,20},{4,12},{0,4},{9,1},{1... | collective-permute-start | bytes 688136 | tf_op jit(solution)/shard_map/ppermute | solution.py:82
  80.3 7.9 %collective-permute-start.12 = (bf16[64,1792]{1,0:T(8,128)(2,1)S(1)}, bf16[64,1792]{1,0:T(8,128)(2,1)S(1)}, u32[]{:S(2)}, u32[]{:S(2)}) collective-permute-start(bf16[64,1792]{1,0:T(8,128)(2,1)S(1)} %collective-permute-done.10), channel_id=1, source_target_pairs={{0,8},{8,16},{16,24},{24,28},{28,20},{20,12},{12,4},{4,0},{1,9},{9... | collective-permute-start | bytes 688136 | tf_op jit(solution)/shard_map/ppermute | solution.py:81
  92.0 40.6 %all-to-all-start.1 = ((bf16[8,1,128,736]{2,3,1,0:T(8,128)(2,1)}), bf16[8,1,128,736]{2,3,1,0:T(8,128)(2,1)S(1)}, u32[]{:S(2)}, u32[]{:S(2)}) async-start(bf16[8,1,128,736]{2,3,1,0:T(8,128)(2,1)} %pad_maximum_fusion), calls=%async_computation.1 | async-start | bytes 3014656 | tf_op jit(solution)/shard_map/all_to_all | solution.py:33
  101.2 14.2 %collective-permute-start.30 = (bf16[128,1792]{1,0:T(8,128)(2,1)S(1)}, bf16[128,1792]{1,0:T(8,128)(2,1)}, u32[]{:S(2)}, u32[]{:S(2)}) collective-permute-start(bf16[128,1792]{1,0:T(8,128)(2,1)S(1)} %fusion), channel_id=1, source_target_pairs={{2,0},{3,1},{6,4},{7,5},{10,8},{11,9},{14,12},{15,13},{18,16},{19,... | collective-permute-start | bytes 1376264 | tf_op jit(solution)/shard_map/ppermute | solution.py:20
  132.6 39.5 %all-to-all-start = ((bf16[8,1,128,736]{2,3,1,0:T(8,128)(2,1)}), bf16[8,1,128,736]{2,3,1,0:T(8,128)(2,1)S(1)}, u32[]{:S(2)}, u32[]{:S(2)}) async-start(bf16[8,1,128,736]{2,3,1,0:T(8,128)(2,1)} %pad_maximum_fusion.1), calls=%async_computation | async-start | bytes 3014656 | tf_op jit(solution)/shard_map/all_to_all | solution.py:33
  138.1 34.5 %collective-permute-start.33 = (bf16[8,1,128,512]{2,3,0,1:T(8,128)(2,1)}, bf16[8,1,128,512]{2,3,0,1:T(8,128)(2,1)}, u32[]{:S(2)}, u32[]{:S(2)}) collective-permute-start(bf16[8,1,128,512]{2,3,0,1:T(8,128)(2,1)} %get-tuple-element.23), channel_id=1, source_target_pairs={{0,1},{1,0},{2,3},{3,2},{4,5},{5,4},{6,7},{7,6},{8,9},{9,8},{10,11... | collective-permute-start | bytes 3145736 | tf_op jit(solution)/shard_map/ppermute | solution.py:14
  178.6 26.7 %all-to-all-start.2 = ((bf16[8,128,448]{1,2,0:T(8,128)(2,1)}), bf16[8,128,448]{1,2,0:T(8,128)(2,1)S(1)}, u32[]{:S(2)}, u32[]{:S(2)}) async-start(bf16[8,128,448]{1,2,0:T(8,128)(2,1)} %pad_maximum_fusion.2), calls=%async_computation.2 | async-start | bytes 1835008 | tf_op jit(solution)/shard_map/all_to_all | solution.py:33
  (20 other events, 238.5 us)
